TPU v7x, 32 devices: a whole 2x2x4 slice. The times are simulated.
32 devices in a mesh: lat: 4 (over y, x), lon: 4 (over z), mem: 2 (over core).
Axes of the slice: x: 2, y: 2, z: 4, core: 2. Of those that a mesh axis runs over, the one named last changes fastest.
Arguments:
- anomalies: bfloat16 [24, 4, 1440, 512], P('mem', None, 'lon', 'lat'), may hold values from -6 to 6
- taper: float32 [4, 1440, 512], P('lon', 'lat'), may hold values from 0.5 to 8
- obs_row: int32 [256, 512], P('lat', 'lon'), may hold values from 0 to 511, as said below
- obs_col: int32 [256, 512], P('lat', 'lon'), may hold values from 0 to 1439, as said below
- obs_level: int32 [256, 512], P('lat', 'lon'), may hold values from 0 to 3
- obs_value: float32 [256, 512], P('lat', 'lon'), may hold values from -18 to 18
Outputs:
- increment: float32 [4, 1440, 512], P(None, 'lon', 'lat')
Inputs may be any that keep to these rules, and one draw needn't show every extreme that they name: `obs_row`: the entry in row i lies in latitude rows (i // 64) * 128 to (i // 64 + 1) * 128 - 1, drawn evenly there. `obs_col`: the entry in column j lies in longitude columns (j // 128) * 360 to (j // 128 + 1) * 360 - 1, drawn evenly there.
All inputs are finite; a program needn't handle non-finite values.
Results may differ from a plain program's by a relative error of at most 0.0066.
Values may be sent and summed in bfloat16 or wider, within the bound.
A program may use at most 128 MiB of HBM per device.

v0:
```python
import math
import jax
import jax.numpy as jnp
from jax import lax
from jax.sharding import PartitionSpec as P


def lon_basis(length):
    grid_idx = jnp.arange(length, dtype=jnp.int32)[:, None]
    coef_idx = jnp.arange(length, dtype=jnp.int32)[None, :]
    nyquist = length // 2
    wavenum = jnp.where(coef_idx <= nyquist, coef_idx, coef_idx - nyquist)
    phase_idx = grid_idx * wavenum % length
    angles = phase_idx.astype(jnp.float32) * (2.0 * math.pi / length)
    scales = jnp.where(
        (coef_idx == 0) | (coef_idx == nyquist), 1.0 / math.sqrt(length), math.sqrt(2.0 / length)
    )
    basis = jnp.where(coef_idx <= nyquist, jnp.cos(angles), jnp.sin(angles)) * scales
    return basis.astype(jnp.bfloat16)


def lat_basis(length):
    grid_idx = jnp.arange(length, dtype=jnp.int32)[:, None]
    mode_idx = jnp.arange(length, dtype=jnp.int32)[None, :]
    phase_idx = mode_idx * (2 * grid_idx + 1) % (4 * length)
    angles = phase_idx.astype(jnp.float32) * (math.pi / (2.0 * length))
    scales = jnp.where(mode_idx == 0, 1.0 / math.sqrt(length), math.sqrt(2.0 / length))
    return (jnp.cos(angles) * scales).astype(jnp.bfloat16)


def spread_observations(cell_keys, row_local, obs_value, slot_count, row_count):
    obs_count = cell_keys.size
    block_rows = min(obs_count, 2048)
    turn_count = obs_count // block_rows
    key_blocks = cell_keys.reshape(turn_count, block_rows)
    row_blocks = row_local.reshape(turn_count, block_rows)
    value_blocks = obs_value.reshape(turn_count, block_rows)
    slot_ids = jnp.arange(slot_count, dtype=jnp.int32)
    row_ids = jnp.arange(row_count, dtype=jnp.int32)

    def add_block(running, obs_block):
        key_part, row_part, value_part = obs_block
        left_hot = (key_part[:, None] == slot_ids[None, :]).astype(jnp.bfloat16)
        high_part = value_part.astype(jnp.bfloat16)
        remainder = value_part - high_part.astype(jnp.float32)
        middle_part = remainder.astype(jnp.bfloat16)
        low_part = (remainder - middle_part.astype(jnp.float32)).astype(jnp.bfloat16)
        pieces = jnp.stack([high_part, middle_part, low_part], axis=1)
        row_hits = (row_part[:, None] == row_ids[None, :]).astype(jnp.bfloat16)
        weighted_rows = (pieces[:, :, None] * row_hits[:, None, :]).reshape(
            block_rows, 3 * row_count
        )
        added = jnp.einsum("ok,oz->kz", left_hot, weighted_rows, preferred_element_type=jnp.float32)
        return (running + added, None)

    start_sum = jnp.zeros((slot_count, 3 * row_count), jnp.float32)
    running, _ = lax.scan(add_block, start_sum, (key_blocks, row_blocks, value_blocks))
    return jnp.sum(running.reshape(slot_count, 3, row_count), axis=1)


def local(anomalies, taper, obs_row, obs_col, obs_level, obs_value):
    member_count, level_count, col_count, row_count = anomalies.shape
    lon_total = col_count * lax.axis_size("lon")
    lat_total = row_count * lax.axis_size("lat")
    row_start = lax.axis_index("lat") * row_count
    col_start = lax.axis_index("lon") * col_count
    cell_keys = (obs_level * col_count + (obs_col - col_start)).reshape(-1)
    row_local = (obs_row - row_start).reshape(-1)
    innovation = spread_observations(
        cell_keys, row_local, obs_value.reshape(-1), level_count * col_count, row_count
    )
    innovation = innovation.reshape(level_count, col_count, row_count).astype(jnp.bfloat16)
    lon_table = lon_basis(lon_total)
    lat_table = lat_basis(lat_total)
    ensemble = member_count * lax.axis_size("mem")
    fields, innov_cols = (
        lax.all_to_all(anomalies, "lon", split_axis=1, concat_axis=2, tiled=True),
        lax.all_to_all(innovation[None], "lon", split_axis=1, concat_axis=2, tiled=True),
    )
    zonal_coef = jnp.einsum(
        "alxy,xk->alky", fields * innov_cols, lon_table, preferred_element_type=jnp.float32
    ).astype(jnp.bfloat16)
    modal_zonal_coef = lax.all_to_all(zonal_coef, "lat", split_axis=2, concat_axis=3, tiled=True)
    spectrum = jnp.einsum(
        "alky,yn->alkn", modal_zonal_coef, lat_table, preferred_element_type=jnp.float32
    )
    tapered = (spectrum * taper[None]).astype(jnp.bfloat16)
    filtered = jnp.einsum(
        "alkn,yn->alky", tapered, lat_table, preferred_element_type=jnp.float32
    ).astype(jnp.bfloat16)
    inverse = lax.all_to_all(filtered, "lat", split_axis=3, concat_axis=2, tiled=True)
    localized = jnp.einsum("alky,xk->alxy", inverse, lon_table, preferred_element_type=jnp.float32)
    local_sum = jnp.sum(fields.astype(jnp.float32) * localized, axis=0)
    merged = lax.psum(local_sum, "mem")
    summed = lax.all_to_all(merged, "lon", split_axis=1, concat_axis=0, tiled=True)
    return summed / (ensemble - 1)


def solution(mesh):
    in_specs = (
        P("mem", None, "lon", "lat"),
        P("lon", "lat", None),
        P("lat", "lon"),
        P("lat", "lon"),
        P("lat", "lon"),
        P("lat", "lon"),
    )
    out_specs = P(None, "lon", "lat")
    return jax.shard_map(local, mesh=mesh, in_specs=in_specs, out_specs=out_specs, check_vma=False)
```

profile of v0, /device:TPU:0, one launch (start us, length us, event | category | flops | bytes accessed | tf_op | source)
XLA Modules:
  0.0 481.3 jit_solution(4805282629353373172)
XLA Ops:
  6.5 4.6 copy.33
  11.1 6.5 %all-to-all-start = ((bf16[12,4,360,128]{3,2,0,1:T(8,128)(2,1)}), bf16[12,4,360,128]{3,2,0,1:T(8,128)(2,1)}, u32[]{:S(2)}, u32[]{:S(2)}) async-start(bf16[12,4,360,128]{3,2,0,1:T(8,128)(2,1)} %copy.33), calls=%async_computation | async-start | bytes 8847360 | tf_op jit(solution)/shard_map/all_to_all | solution.py:77
  17.6 0.0 copy-done.2
  17.6 0.0 copy-done
  17.6 0.0 copy-done.1
  17.7 0.0 copy-done.3
  17.7 27.3 %while.11 = (s32[]{:T(128)}, f32[1440,384]{1,0:T(8,128)}, s32[4,2048]{1,0:T(4,128)S(1)}, f32[4,2048]{1,0:T(4,128)S(1)}, s32[4,2048]{1,0:T(4,128)S(1)}, /*index=5*/s32[]{:T(128)}, s32[]{:T(128)}) while((s32[]{:T(128)}, f32[1440,384]{1,0:T(8,128)}, s32[4,2048]{1,0:T(4,128)S(1)}, f32[4,2048]{1,0:T(4,128)S(1)}, ...), condition=%wide.region_1.2_spmd.clone, body=%wide.region_0.1_spmd.clone.sunk | while | flops 2273290240 | bytes 8728675 | solution.py:57
  17.9 0.1 fusion.93
  18.0 0.1 broadcast_multiply_fusion.3
  18.1 5.2 %fusion.95 = f32[1440,384]{1,0:T(8,128)} fusion(bf16[2048,384]{0,1:T(8,128)(2,1)S(1)} %bitcast.84, s32[2048]{0:T(1024)S(1)} %bitcast.91, f32[1440,384]{1,0:T(8,128)} %get-tuple-element.126, pred[]{:T(512)S(6)} %compare.4), kind=kOutput, calls=%fused_computation.6.clone.1 | convolution fusion | flops 2271928320 | bytes 6004737 | tf_op jit(solution)/shard_map/while/body/eval_jaxpr/ok,oz->kz/dot_general | solution.py:53
  23.5 0.1 fusion.93
  23.6 0.1 broadcast_multiply_fusion.3
  23.7 6.8 %fusion.95 = f32[1440,384]{1,0:T(8,128)} fusion(bf16[2048,384]{0,1:T(8,128)(2,1)S(1)} %bitcast.84, s32[2048]{0:T(1024)S(1)} %bitcast.91, f32[1440,384]{1,0:T(8,128)} %get-tuple-element.126, pred[]{:T(512)S(6)} %compare.4), kind=kOutput, calls=%fused_computation.6.clone.1 | convolution fusion | flops 2271928320 | bytes 6004737 | tf_op jit(solution)/shard_map/while/body/eval_jaxpr/ok,oz->kz/dot_general | solution.py:53
  30.7 0.1 fusion.93
  30.8 0.1 broadcast_multiply_fusion.3
  30.9 6.9 %fusion.95 = f32[1440,384]{1,0:T(8,128)} fusion(bf16[2048,384]{0,1:T(8,128)(2,1)S(1)} %bitcast.84, s32[2048]{0:T(1024)S(1)} %bitcast.91, f32[1440,384]{1,0:T(8,128)} %get-tuple-element.126, pred[]{:T(512)S(6)} %compare.4), kind=kOutput, calls=%fused_computation.6.clone.1 | convolution fusion | flops 2271928320 | bytes 6004737 | tf_op jit(solution)/shard_map/while/body/eval_jaxpr/ok,oz->kz/dot_general | solution.py:53
  37.9 0.1 fusion.93
  38.0 0.1 broadcast_multiply_fusion.3
  38.2 6.8 %fusion.95 = f32[1440,384]{1,0:T(8,128)} fusion(bf16[2048,384]{0,1:T(8,128)(2,1)S(1)} %bitcast.84, s32[2048]{0:T(1024)S(1)} %bitcast.91, f32[1440,384]{1,0:T(8,128)} %get-tuple-element.126, pred[]{:T(512)S(6)} %compare.4), kind=kOutput, calls=%fused_computation.6.clone.1 | convolution fusion | flops 2271928320 | bytes 6004737 | tf_op jit(solution)/shard_map/while/body/eval_jaxpr/ok,oz->kz/dot_general | solution.py:53
  45.0 2.0 copy.36
  47.0 0.2 reduce_sum.20
  47.3 0.9 copy.37
  48.2 67.8 %all-to-all-done = bf16[12,4,360,128]{3,2,0,1:T(8,128)(2,1)} async-done(((bf16[12,4,360,128]{3,2,0,1:T(8,128)(2,1)}), bf16[12,4,360,128]{3,2,0,1:T(8,128)(2,1)}, u32[]{:S(2)}, u32[]{:S(2)}) %all-to-all-start) | async-done | bytes 4423712 | tf_op jit(solution)/shard_map/all_to_all | solution.py:77
  116.0 3.9 all-to-all-start.1
  119.9 39.0 %fusion.84 = bf16[1440,1440,1]{1,0,2:T(8,128)(2,1)} fusion(f32[1440]{0:T(1024)S(1)} %fusion.58, s32[1440]{0:T(1024)S(1)} %add_select_fusion.2, pred[1440]{0:T(1024)(128)(4,1)S(1)} %iota_compare_fusion.4), kind=kLoop, calls=%fused_computation.29.clone.clone.clone.clone.1 | loop fusion | flops 24883200 | bytes 4160160 | tf_op jit(solution)/shard_map/alxy,xk->alky/dot_general | solution.py:80
  158.9 4.7 copy.35
  163.6 0.0 all-to-all-done.1
  163.6 2.9 bitcast_multiply_fusion.1
  166.5 0.7 copy-done.5
  167.2 7.6 %fusion.28 = bf16[12,1,1440,128]{3,2,0,1:T(8,128)(2,1)S(1)} fusion(bf16[12,1440,128]{2,1,0:T(8,128)(2,1)S(1)} %bitcast_multiply_fusion.1, bf16[1440,1440,1]{1,0,2:T(8,128)(2,1)S(1)} %copy-done.5), kind=kOutput, calls=%fused_computation.39 | convolution fusion | flops 6372311040 | bytes 12994560 | tf_op jit(solution)/shard_map/alxy,xk->alky/dot_general | solution.py:80
  174.8 12.3 %copy.40 = bf16[12,1,1440,128]{3,0,1,2:T(8,128)(2,1)} copy(bf16[12,1,1440,128]{3,2,0,1:T(8,128)(2,1)S(1)} %fusion.28) | data formatting | bytes 8847360 | tf_op jit(solution)/shard_map/convert_element_type | solution.py:82
  187.1 5.2 %all-to-all-start.2 = ((bf16[12,1,1440,128]{3,0,1,2:T(8,128)(2,1)}), bf16[12,1,1440,128]{3,0,1,2:T(8,128)(2,1)}, u32[]{:S(2)}, u32[]{:S(2)}) async-start(bf16[12,1,1440,128]{3,0,1,2:T(8,128)(2,1)} %copy.40), calls=%async_computation.2 | async-start | bytes 11796480 | tf_op jit(solution)/shard_map/all_to_all | solution.py:83
  192.3 65.0 %all-to-all-done.2 = bf16[12,1,1440,128]{3,0,1,2:T(8,128)(2,1)} async-done(((bf16[12,1,1440,128]{3,0,1,2:T(8,128)(2,1)}), bf16[12,1,1440,128]{3,0,1,2:T(8,128)(2,1)}, u32[]{:S(2)}, u32[]{:S(2)}) %all-to-all-start.2) | async-done | bytes 4423712 | tf_op jit(solution)/shard_map/all_to_all | solution.py:83
  257.3 8.2 %copy.47 = bf16[12,1,4,360,128]{4,2,3,0,1:T(4,128)(2,1)} copy(bf16[12,1,4,360,128]{4,0,3,2,1:T(8,128)(2,1)} %bitcast.10) | data formatting | bytes 8847360 | tf_op jit(solution)/shard_map/all_to_all | solution.py:83
  265.5 8.6 %reshape.193 = bf16[12,360,512]{2,1,0:T(8,128)(2,1)} reshape(bf16[12,1,360,4,128]{4,3,2,0,1:T(4,128)(2,1)} %bitcast.85) | data formatting | bytes 8847360 | tf_op jit(solution)/shard_map/reshape.13
  274.1 0.0 copy-done.4
  274.1 16.1 %convert_bitcast_fusion = bf16[12,1,360,512]{3,2,0,1:T(8,128)(2,1)} fusion(f32[360,512]{1,0:T(8,128)S(1)} %bitcast.92, bf16[12,360,512]{2,1,0:T(8,128)(2,1)} %reshape.193, f32[512]{0:T(512)S(1)} %fusion.59, s32[512]{0:T(512)S(1)} %multiply_add_fusion), kind=kOutput, calls=%fused_computation.33 | convolution fusion | flops 4544872448 | bytes 9588736 | tf_op jit(solution)/shard_map/alkn,yn->alky/dot_general | solution.py:88
  290.2 8.9 %copy.42 = bf16[12,1,360,512]{2,0,1,3:T(8,128)(2,1)} copy(bf16[12,1,360,512]{3,2,0,1:T(8,128)(2,1)} %convert_bitcast_fusion) | data formatting | bytes 8847360 | tf_op jit(solution)/shard_map/convert_element_type | solution.py:90
  299.2 5.2 %all-to-all-start.3 = ((bf16[12,1,360,512]{2,0,1,3:T(8,128)(2,1)}), bf16[12,1,360,512]{2,0,1,3:T(8,128)(2,1)}, u32[]{:S(2)}, u32[]{:S(2)}) async-start(bf16[12,1,360,512]{2,0,1,3:T(8,128)(2,1)} %copy.42), calls=%async_computation.3 | async-start | bytes 12582912 | tf_op jit(solution)/shard_map/all_to_all | solution.py:91
  304.4 0.0 all-reduce.2.cloned.1.call-start
  304.5 6.4 %copy.34 = f32[12,4,360,128]{3,2,1,0:T(8,128)} copy(bf16[12,4,360,128]{3,2,0,1:T(8,128)(2,1)} %all-to-all-done) | data formatting | bytes 13271040 | tf_op jit(solution)/shard_map/convert_element_type | solution.py:93
  310.9 62.9 %all-to-all-done.3 = bf16[12,1,360,512]{2,0,1,3:T(8,128)(2,1)} async-done(((bf16[12,1,360,512]{2,0,1,3:T(8,128)(2,1)}), bf16[12,1,360,512]{2,0,1,3:T(8,128)(2,1)}, u32[]{:S(2)}, u32[]{:S(2)}) %all-to-all-start.3) | async-done | bytes 4423712 | tf_op jit(solution)/shard_map/all_to_all | solution.py:91
  373.8 8.8 %copy.43 = bf16[12,1,360,4,128]{4,2,3,0,1:T(8,128)(2,1)} copy(bf16[12,1,360,4,128]{2,0,4,3,1:T(8,128)(2,1)} %bitcast.15) | data formatting | bytes 8847360 | tf_op jit(solution)/shard_map/all_to_all | solution.py:91
  382.5 46.6 %fusion.15 = f32[1440,128]{1,0:T(8,128)} fusion(f32[12,4,360,128]{3,2,1,0:T(8,128)} %copy.34, bf16[12,1440,128]{2,1,0:T(8,128)(2,1)} %bitcast.87, f32[1440]{0:T(1024)S(1)} %fusion.58, s32[1440]{0:T(1024)S(1)} %add_select_fusion.2, pred[1440]{0:T(1024)(128)(4,1)S(1)} %iota_compare_fusion.4), kind=kOutput, calls=%fused_computation.21 | convolution fusion | flops 6399221760 | bytes 14021280 | tf_op jit(solution)/shard_map/alky,xk->alxy/dot_general | solution.py:92
  429.1 0.0 all-reduce.2.cloned.1.call-update
  429.1 19.2 %all-reduce.2.cloned.1.call-done = f32[1,1440,128]{2,0,1:T(1,128)} async-done(((f32[1,1440,128]{2,0,1:T(1,128)}), f32[1,1440,128]{2,0,1:T(1,128)}) %all-reduce.2.cloned.1.call-update) | async-done | bytes 737296 | tf_op jit(solution)/shard_map/psum | solution.py:94
  448.3 24.4 %all_to_all.60 = f32[1,1440,128]{2,0,1:T(1,128)S(1)} all-to-all(f32[1,1440,128]{2,0,1:T(1,128)} %all-reduce.2.cloned.1.call-done), channel_id=1, replica_groups=mesh['lat'=4,'lon'=4,'mem'=2] {'lon'}, dimensions={1} | all-to-all | bytes 1474560 | tf_op jit(solution)/shard_map/all_to_all | solution.py:95
  472.7 1.5 broadcast_multiply_fusion.1
  (33 shorter events, 0.5 us)
Async XLA Ops:
  11.1 6.5 %copy-start.2 = (s32[64,128]{1,0:T(8,128)S(1)}, s32[64,128]{1,0:T(8,128)}, u32[]{:S(2)}) copy-start(s32[64,128]{1,0:T(8,128)} %param.10) | copy-start | bytes 98308
  11.1 6.5 %copy-start = (s32[64,128]{1,0:T(8,128)S(1)}, s32[64,128]{1,0:T(8,128)}, u32[]{:S(2)}) copy-start(s32[64,128]{1,0:T(8,128)} %param.11) | copy-start | bytes 98308
  11.1 6.5 %copy-start.1 = (s32[64,128]{1,0:T(8,128)S(1)}, s32[64,128]{1,0:T(8,128)}, u32[]{:S(2)}) copy-start(s32[64,128]{1,0:T(8,128)} %param.12) | copy-start | bytes 98308
  11.1 6.6 %copy-start.3 = (f32[64,128]{1,0:T(8,128)S(1)}, f32[64,128]{1,0:T(8,128)}, u32[]{:S(2)}) copy-start(f32[64,128]{1,0:T(8,128)} %param.13) | copy-start | bytes 98308
  11.1 104.9 %all-to-all-start = ((bf16[12,4,360,128]{3,2,0,1:T(8,128)(2,1)}), bf16[12,4,360,128]{3,2,0,1:T(8,128)(2,1)}, u32[]{:S(2)}, u32[]{:S(2)}) async-start(bf16[12,4,360,128]{3,2,0,1:T(8,128)(2,1)} %copy.33), calls=%async_computation | async-start | bytes 8847360 | tf_op jit(solution)/shard_map/all_to_all | solution.py:77
  116.0 47.6 %all-to-all-start.1 = ((bf16[1,4,360,128]{3,2,0,1:T(8,128)(2,1)}), bf16[1,4,360,128]{3,2,0,1:T(8,128)(2,1)S(1)}, u32[]{:S(2)}, u32[]{:S(2)}) async-start(bf16[1,4,360,128]{3,2,0,1:T(8,128)(2,1)} %bitcast.6), calls=%async_computation.1 | async-start | bytes 737280 | tf_op jit(solution)/shard_map/all_to_all | solution.py:78
  163.6 3.6 copy-start.5
  187.1 70.2 %all-to-all-start.2 = ((bf16[12,1,1440,128]{3,0,1,2:T(8,128)(2,1)}), bf16[12,1,1440,128]{3,0,1,2:T(8,128)(2,1)}, u32[]{:S(2)}, u32[]{:S(2)}) async-start(bf16[12,1,1440,128]{3,0,1,2:T(8,128)(2,1)} %copy.40), calls=%async_computation.2 | async-start | bytes 11796480 | tf_op jit(solution)/shard_map/all_to_all | solution.py:83
  265.5 8.6 %copy-start.4 = (f32[1,360,512]{2,1,0:T(8,128)S(1)}, f32[1,360,512]{2,1,0:T(8,128)}, u32[]{:S(2)}) copy-start(f32[1,360,512]{2,1,0:T(8,128)} %param.9) | copy-start | bytes 2211844
  299.2 74.6 %all-to-all-start.3 = ((bf16[12,1,360,512]{2,0,1,3:T(8,128)(2,1)}), bf16[12,1,360,512]{2,0,1,3:T(8,128)(2,1)}, u32[]{:S(2)}, u32[]{:S(2)}) async-start(bf16[12,1,360,512]{2,0,1,3:T(8,128)(2,1)} %copy.42), calls=%async_computation.3 | async-start | bytes 12582912 | tf_op jit(solution)/shard_map/all_to_all | solution.py:91
  304.4 143.9 %all-reduce.2.cloned.1.call-start = ((), (), s32[]{:S(2)}) async-start(), calls=%async_computation.5 | async-start | bytes 1474560 | tf_op jit(solution)/shard_map/psum | solution.py:94
Sparse Core Ops, SparseCore 0:
  429.2 19.0 all-reduce.1
where the time goes:
time: 487 us; the launch traced here: 481 us
  waiting for transfers between devices  215 us (44%)
  matrix products  96 us (20%)
  local copies, waits for them, and re-layouts  66.3 us (14%)
  other arithmetic  44.8 us (9%)
  blocking collectives  24.4 us (5%)
  starting transfers between devices  20.9 us (4%)
  between operations  13.8 us (3%)
    all_to_all x1, waiting for transfers between devices, local(): lax.all_to_all(anomalies, 'lon', split_axis=1, concat_axis=2, tiled=True)  67.8 us
    all_to_all x1, waiting for transfers between devices, local(): lax.all_to_all(zonal_coef, 'lat', split_axis=2, concat_axis=3, tiled=True)  65 us
    all_to_all x1, waiting for transfers between devices, local(): lax.all_to_all(filtered, 'lat', split_axis=3, concat_axis=2, tiled=True)  62.9 us
    dot_general x1, matrix products, local(): jnp.einsum('alky,xk->alxy', inverse, lon_table, preferred_element_type=jn...  46.6 us
    dot_general x1, other arithmetic, local(): jnp.einsum('alxy,xk->alky', fields * innov_cols, lon_table, preferred_ele...  39 us
    dot_general x4, matrix products, add_block(): jnp.einsum('ok,oz->kz', left_hot, weighted_rows, preferred_element_type=j...  25.7 us
    all_to_all x1, blocking collectives, local(): lax.all_to_all(merged, 'lon', split_axis=1, concat_axis=0, tiled=True)  24.4 us
    psum x1, waiting for transfers between devices, local(): merged = lax.psum(local_sum, 'mem')  19.2 us
  transfers between devices with their start and end apart: 5, of which 4 were waited for; matrix products, arithmetic and copies ran while one was open for 17% of the time, Pallas kernels for 0%

commit v1 on v0

--- a/solution.py
+++ b/solution.py
@@ -88,7 +88,10 @@
     filtered = jnp.einsum(
         "alkn,yn->alky", tapered, lat_table, preferred_element_type=jnp.float32
     ).astype(jnp.bfloat16)
-    inverse = lax.all_to_all(filtered, "lat", split_axis=3, concat_axis=2, tiled=True)
+    peers = lax.axis_size("lat")
+    blocks = jnp.stack(jnp.split(filtered, peers, axis=3), axis=0)
+    blocks = lax.all_to_all(blocks, "lat", split_axis=0, concat_axis=0)
+    inverse = jnp.concatenate(blocks, axis=2)
     localized = jnp.einsum("alky,xk->alxy", inverse, lon_table, preferred_element_type=jnp.float32)
     local_sum = jnp.sum(fields.astype(jnp.float32) * localized, axis=0)
     merged = lax.psum(local_sum, "mem")

time: 487 us -> 456 us (0.936)
  waiting for transfers between devices: 215 us -> 195 us
  local copies, waits for them, and re-layouts: 66.3 us -> 56.2 us
    all_to_all x1, waiting for transfers between devices: 62.9 us -> 42.7 us  [local(): blocks = lax.all_to_all(blocks, 'lat', split_axis=0, concat_axis=0)]
    convert_element_type x1 -> x0, local copies, waits for them, and re-layouts: 8.94 us -> none  [local(): filtered = jnp.einsum('alkn,yn->alky', tapered, lat_table, preferred_elem...]
    all_to_all x1 -> x0, local copies, waits for them, and re-layouts: 8.75 us -> none  [local(): lax.all_to_all(filtered, 'lat', split_axis=3, concat_axis=2, tiled=True)]
    another operation x1 -> x2, local copies, waits for them, and re-layouts: 8.6 us -> 11.1 us
  transfers between devices with their start and end apart: 5 -> 5, of which waited for: 4 -> 4; matrix products, arithmetic and copies ran while one was open for 17% -> 18% of each run, Pallas kernels for 0% -> 0%
where the time goes in v1:
time: 456 us; the launch traced here: 451 us
  waiting for transfers between devices  195 us (43%)
  matrix products  93.3 us (20%)
  local copies, waits for them, and re-layouts  56.2 us (12%)
  other arithmetic  47.1 us (10%)
  blocking collectives  24.4 us (5%)
  starting transfers between devices  20.9 us (5%)
  between operations  13.8 us (3%)
    all_to_all x1, waiting for transfers between devices, local(): lax.all_to_all(anomalies, 'lon', split_axis=1, concat_axis=2, tiled=True)  67.9 us
    all_to_all x1, waiting for transfers between devices, local(): lax.all_to_all(zonal_coef, 'lat', split_axis=2, concat_axis=3, tiled=True)  65.1 us
    dot_general x1, matrix products, local(): jnp.einsum('alky,xk->alxy', inverse, lon_table, preferred_element_type=jn...  43.9 us
    all_to_all x1, waiting for transfers between devices, local(): blocks = lax.all_to_all(blocks, 'lat', split_axis=0, concat_axis=0)  42.7 us
    dot_general x1, other arithmetic, local(): jnp.einsum('alxy,xk->alky', fields * innov_cols, lon_table, preferred_ele...  39 us
    dot_general x4, matrix products, add_block(): jnp.einsum('ok,oz->kz', left_hot, weighted_rows, preferred_element_type=j...  25.6 us
    all_to_all x1, blocking collectives, local(): lax.all_to_all(merged, 'lon', split_axis=1, concat_axis=0, tiled=True)  24.4 us
    psum x1, waiting for transfers between devices, local(): merged = lax.psum(local_sum, 'mem')  19.2 us
  transfers between devices with their start and end apart: 5, of which 4 were waited for; matrix products, arithmetic and copies ran while one was open for 18% of the time, Pallas kernels for 0%

profile of v1, /device:TPU:0, one launch (start us, length us, event | category | flops | bytes accessed | tf_op | source)
XLA Modules:
  0.0 450.8 jit_solution(1033809555501160238)
XLA Ops:
  6.5 4.7 %copy.30 = bf16[12,4,360,128]{3,2,0,1:T(8,128)(2,1)} copy(bf16[12,4,360,128]{3,2,1,0:T(8,128)(2,1)} %param.8) | data formatting | bytes 8847360 | tf_op args[0]
  11.2 6.5 %all-to-all-start = ((bf16[12,4,360,128]{3,2,0,1:T(8,128)(2,1)}), bf16[12,4,360,128]{3,2,0,1:T(8,128)(2,1)}, u32[]{:S(2)}, u32[]{:S(2)}) async-start(bf16[12,4,360,128]{3,2,0,1:T(8,128)(2,1)} %copy.30), calls=%async_computation | async-start | bytes 8847360 | tf_op jit(solution)/shard_map/all_to_all | solution.py:77
  17.7 0.0 copy-done.1
  17.7 0.0 copy-done.2
  17.8 0.0 copy-done.4
  17.8 27.1 %while.11 = (s32[]{:T(128)}, f32[1440,384]{1,0:T(8,128)}, s32[4,2048]{1,0:T(4,128)S(1)}, f32[4,2048]{1,0:T(4,128)S(1)}, s32[4,2048]{1,0:T(4,128)S(1)}, /*index=5*/s32[]{:T(128)}, s32[]{:T(128)}) while((s32[]{:T(128)}, f32[1440,384]{1,0:T(8,128)}, s32[4,2048]{1,0:T(4,128)S(1)}, f32[4,2048]{1,0:T(4,128)S(1)}, ...), condition=%wide.region_1.2_spmd.clone, body=%wide.region_0.1_spmd.clone.sunk | while | flops 2273290240 | bytes 8728675 | solution.py:57
  18.0 0.1 fusion.93
  18.1 0.1 broadcast_multiply_fusion.3
  18.2 5.2 %fusion.95 = f32[1440,384]{1,0:T(8,128)} fusion(bf16[2048,384]{0,1:T(8,128)(2,1)S(1)} %bitcast.90, s32[2048]{0:T(1024)S(1)} %bitcast.97, f32[1440,384]{1,0:T(8,128)} %get-tuple-element.130, pred[]{:T(512)S(6)} %compare.4), kind=kOutput, calls=%fused_computation.6.clone.1 | convolution fusion | flops 2271928320 | bytes 6004737 | tf_op jit(solution)/shard_map/while/body/eval_jaxpr/ok,oz->kz/dot_general | solution.py:53
  23.5 0.1 fusion.93
  23.6 0.1 broadcast_multiply_fusion.3
  23.8 6.8 %fusion.95 = f32[1440,384]{1,0:T(8,128)} fusion(bf16[2048,384]{0,1:T(8,128)(2,1)S(1)} %bitcast.90, s32[2048]{0:T(1024)S(1)} %bitcast.97, f32[1440,384]{1,0:T(8,128)} %get-tuple-element.130, pred[]{:T(512)S(6)} %compare.4), kind=kOutput, calls=%fused_computation.6.clone.1 | convolution fusion | flops 2271928320 | bytes 6004737 | tf_op jit(solution)/shard_map/while/body/eval_jaxpr/ok,oz->kz/dot_general | solution.py:53
  30.7 0.1 fusion.93
  30.8 0.1 broadcast_multiply_fusion.3
  31.0 6.8 %fusion.95 = f32[1440,384]{1,0:T(8,128)} fusion(bf16[2048,384]{0,1:T(8,128)(2,1)S(1)} %bitcast.90, s32[2048]{0:T(1024)S(1)} %bitcast.97, f32[1440,384]{1,0:T(8,128)} %get-tuple-element.130, pred[]{:T(512)S(6)} %compare.4), kind=kOutput, calls=%fused_computation.6.clone.1 | convolution fusion | flops 2271928320 | bytes 6004737 | tf_op jit(solution)/shard_map/while/body/eval_jaxpr/ok,oz->kz/dot_general | solution.py:53
  37.9 0.1 fusion.93
  38.0 0.1 broadcast_multiply_fusion.3
  38.1 6.8 %fusion.95 = f32[1440,384]{1,0:T(8,128)} fusion(bf16[2048,384]{0,1:T(8,128)(2,1)S(1)} %bitcast.90, s32[2048]{0:T(1024)S(1)} %bitcast.97, f32[1440,384]{1,0:T(8,128)} %get-tuple-element.130, pred[]{:T(512)S(6)} %compare.4), kind=kOutput, calls=%fused_computation.6.clone.1 | convolution fusion | flops 2271928320 | bytes 6004737 | tf_op jit(solution)/shard_map/while/body/eval_jaxpr/ok,oz->kz/dot_general | solution.py:53
  44.9 2.0 copy.33
  47.0 0.2 reduce_sum.20
  47.2 0.9 copy.34
  48.2 67.9 %all-to-all-done = bf16[12,4,360,128]{3,2,0,1:T(8,128)(2,1)} async-done(((bf16[12,4,360,128]{3,2,0,1:T(8,128)(2,1)}), bf16[12,4,360,128]{3,2,0,1:T(8,128)(2,1)}, u32[]{:S(2)}, u32[]{:S(2)}) %all-to-all-start) | async-done | bytes 4423712 | tf_op jit(solution)/shard_map/all_to_all | solution.py:77
  116.1 3.9 all-to-all-start.1
  120.0 39.0 %fusion.84 = bf16[1440,1440,1]{1,0,2:T(8,128)(2,1)} fusion(f32[1440]{0:T(1024)S(1)} %fusion.58, s32[1440]{0:T(1024)S(1)} %add_select_fusion.2, pred[1440]{0:T(1024)(128)(4,1)S(1)} %iota_compare_fusion.4), kind=kLoop, calls=%fused_computation.29.clone.clone.clone.clone.1 | loop fusion | flops 24883200 | bytes 4160160 | tf_op jit(solution)/shard_map/alxy,xk->alky/dot_general | solution.py:80
  159.0 4.7 %copy.32 = bf16[12,4,360,128]{3,2,1,0:T(8,128)(2,1)} copy(bf16[12,4,360,128]{3,2,0,1:T(8,128)(2,1)} %all-to-all-done) | data formatting | bytes 8847360 | tf_op jit(solution)/shard_map/all_to_all | solution.py:77
  163.7 0.0 all-to-all-done.1
  163.7 2.9 bitcast_multiply_fusion.1
  166.6 0.7 copy-done.6
  167.3 7.6 %fusion.28 = bf16[12,1,1440,128]{3,2,0,1:T(8,128)(2,1)S(1)} fusion(bf16[12,1440,128]{2,1,0:T(8,128)(2,1)S(1)} %bitcast_multiply_fusion.1, bf16[1440,1440,1]{1,0,2:T(8,128)(2,1)S(1)} %copy-done.6), kind=kOutput, calls=%fused_computation.40 | convolution fusion | flops 6372311040 | bytes 12994560 | tf_op jit(solution)/shard_map/alxy,xk->alky/dot_general | solution.py:80
  174.9 12.3 %copy.37 = bf16[12,1,1440,128]{3,0,1,2:T(8,128)(2,1)} copy(bf16[12,1,1440,128]{3,2,0,1:T(8,128)(2,1)S(1)} %fusion.28) | data formatting | bytes 8847360 | tf_op jit(solution)/shard_map/convert_element_type | solution.py:82
  187.2 5.4 %all-to-all-start.2 = ((bf16[12,1,1440,128]{3,0,1,2:T(8,128)(2,1)}), bf16[12,1,1440,128]{3,0,1,2:T(8,128)(2,1)}, u32[]{:S(2)}, u32[]{:S(2)}) async-start(bf16[12,1,1440,128]{3,0,1,2:T(8,128)(2,1)} %copy.37), calls=%async_computation.2 | async-start | bytes 11796480 | tf_op jit(solution)/shard_map/all_to_all | solution.py:83
  192.7 65.1 %all-to-all-done.2 = bf16[12,1,1440,128]{3,0,1,2:T(8,128)(2,1)} async-done(((bf16[12,1,1440,128]{3,0,1,2:T(8,128)(2,1)}), bf16[12,1,1440,128]{3,0,1,2:T(8,128)(2,1)}, u32[]{:S(2)}, u32[]{:S(2)}) %all-to-all-start.2) | async-done | bytes 4423712 | tf_op jit(solution)/shard_map/all_to_all | solution.py:83
  257.8 8.2 %copy.43 = bf16[12,1,4,360,128]{4,2,3,0,1:T(4,128)(2,1)} copy(bf16[12,1,4,360,128]{4,0,3,2,1:T(8,128)(2,1)} %bitcast.10) | data formatting | bytes 8847360 | tf_op jit(solution)/shard_map/all_to_all | solution.py:83
  266.0 8.5 %reshape.197 = bf16[12,360,512]{2,1,0:T(8,128)(2,1)} reshape(bf16[12,1,360,4,128]{4,3,2,0,1:T(4,128)(2,1)} %bitcast.91) | data formatting | bytes 8847360 | tf_op jit(solution)/shard_map/reshape.15
  274.5 16.1 %convert_bitcast_fusion = bf16[12,1,360,512]{3,2,0,1:T(8,128)(2,1)} fusion(f32[360,512]{1,0:T(8,128)S(1)} %bitcast.98, bf16[12,360,512]{2,1,0:T(8,128)(2,1)} %reshape.197, f32[512]{0:T(512)S(1)} %fusion.59, s32[512]{0:T(512)S(1)} %multiply_add_fusion), kind=kOutput, calls=%fused_computation.34 | convolution fusion | flops 4544872448 | bytes 9588736 | tf_op jit(solution)/shard_map/alkn,yn->alky/dot_general | solution.py:88
  290.6 2.6 slice_bitcast_fusion.3
  293.2 2.4 pad_maximum_fusion.1
  295.5 4.9 %all-to-all-start.3 = ((bf16[4,12,1,360,128]{4,3,1,2,0:T(8,128)(2,1)}), bf16[4,12,1,360,128]{4,3,1,2,0:T(8,128)(2,1)}, u32[]{:S(2)}, u32[]{:S(2)}) async-start(bf16[4,12,1,360,128]{4,3,1,2,0:T(8,128)(2,1)} %pad_maximum_fusion.1), calls=%async_computation.3 | async-start | bytes 8847360 | tf_op jit(solution)/shard_map/all_to_all | solution.py:93
  300.4 0.3 all-reduce.2.cloned.1.call-start
  300.7 6.5 %copy.31 = f32[12,4,360,128]{3,2,1,0:T(8,128)} copy(bf16[12,4,360,128]{3,2,0,1:T(8,128)(2,1)} %all-to-all-done) | data formatting | bytes 13271040 | tf_op jit(solution)/shard_map/convert_element_type | solution.py:96
  307.2 42.7 %all-to-all-done.3 = bf16[4,12,1,360,128]{4,3,1,2,0:T(8,128)(2,1)} async-done(((bf16[4,12,1,360,128]{4,3,1,2,0:T(8,128)(2,1)}), bf16[4,12,1,360,128]{4,3,1,2,0:T(8,128)(2,1)}, u32[]{:S(2)}, u32[]{:S(2)}) %all-to-all-start.3) | async-done | bytes 4423712 | tf_op jit(solution)/shard_map/all_to_all | solution.py:93
  349.8 2.7 copy.39
  352.5 2.1 copy-done
  354.7 43.9 %fusion.15 = f32[1440,128]{1,0:T(8,128)} fusion(f32[12,4,360,128]{3,2,1,0:T(8,128)S(1)} %copy-done, bf16[12,1440,128]{2,1,0:T(8,128)(2,1)S(1)} %bitcast.93, f32[1440]{0:T(1024)S(1)} %fusion.58, s32[1440]{0:T(1024)S(1)} %add_select_fusion.2, pred[1440]{0:T(1024)(128)(4,1)S(1)} %iota_compare_fusion.4), kind=kOutput, calls=%fused_computation.21 | convolution fusion | flops 6399221760 | bytes 14021280 | tf_op jit(solution)/shard_map/alky,xk->alxy/dot_general | solution.py:95
  398.6 0.0 all-reduce.2.cloned.1.call-update
  398.6 19.2 %all-reduce.2.cloned.1.call-done = f32[1,1440,128]{2,0,1:T(1,128)} async-done(((f32[1,1440,128]{2,0,1:T(1,128)}), f32[1,1440,128]{2,0,1:T(1,128)}) %all-reduce.2.cloned.1.call-update) | async-done | bytes 737296 | tf_op jit(solution)/shard_map/psum | solution.py:97
  417.9 24.4 %all_to_all.50 = f32[1,1440,128]{2,0,1:T(1,128)S(1)} all-to-all(f32[1,1440,128]{2,0,1:T(1,128)} %all-reduce.2.cloned.1.call-done), channel_id=1, replica_groups=mesh['lat'=4,'lon'=4,'mem'=2] {'lon'}, dimensions={1} | all-to-all | bytes 1474560 | tf_op jit(solution)/shard_map/all_to_all | solution.py:98
  442.3 1.5 broadcast_multiply_fusion.1
  (36 shorter events, 0.5 us)
Async XLA Ops:
  11.2 6.5 %copy-start.3 = (s32[64,128]{1,0:T(8,128)S(1)}, s32[64,128]{1,0:T(8,128)}, u32[]{:S(2)}) copy-start(s32[64,128]{1,0:T(8,128)} %param.10) | copy-start | bytes 98308
  11.2 6.5 %copy-start.1 = (s32[64,128]{1,0:T(8,128)S(1)}, s32[64,128]{1,0:T(8,128)}, u32[]{:S(2)}) copy-start(s32[64,128]{1,0:T(8,128)} %param.11) | copy-start | bytes 98308
  11.2 6.5 %copy-start.2 = (s32[64,128]{1,0:T(8,128)S(1)}, s32[64,128]{1,0:T(8,128)}, u32[]{:S(2)}) copy-start(s32[64,128]{1,0:T(8,128)} %param.12) | copy-start | bytes 98308
  11.2 6.6 %copy-start.4 = (f32[64,128]{1,0:T(8,128)S(1)}, f32[64,128]{1,0:T(8,128)}, u32[]{:S(2)}) copy-start(f32[64,128]{1,0:T(8,128)} %param.13) | copy-start | bytes 98308
  11.2 104.9 %all-to-all-start = ((bf16[12,4,360,128]{3,2,0,1:T(8,128)(2,1)}), bf16[12,4,360,128]{3,2,0,1:T(8,128)(2,1)}, u32[]{:S(2)}, u32[]{:S(2)}) async-start(bf16[12,4,360,128]{3,2,0,1:T(8,128)(2,1)} %copy.30), calls=%async_computation | async-start | bytes 8847360 | tf_op jit(solution)/shard_map/all_to_all | solution.py:77
  116.1 47.6 %all-to-all-start.1 = ((bf16[1,4,360,128]{3,2,0,1:T(8,128)(2,1)}), bf16[1,4,360,128]{3,2,0,1:T(8,128)(2,1)S(1)}, u32[]{:S(2)}, u32[]{:S(2)}) async-start(bf16[1,4,360,128]{3,2,0,1:T(8,128)(2,1)} %bitcast.6), calls=%async_computation.1 | async-start | bytes 737280 | tf_op jit(solution)/shard_map/all_to_all | solution.py:78
  163.7 3.6 copy-start.6
  187.2 70.5 %all-to-all-start.2 = ((bf16[12,1,1440,128]{3,0,1,2:T(8,128)(2,1)}), bf16[12,1,1440,128]{3,0,1,2:T(8,128)(2,1)}, u32[]{:S(2)}, u32[]{:S(2)}) async-start(bf16[12,1,1440,128]{3,0,1,2:T(8,128)(2,1)} %copy.37), calls=%async_computation.2 | async-start | bytes 11796480 | tf_op jit(solution)/shard_map/all_to_all | solution.py:83
  266.0 8.5 %copy-start.5 = (f32[1,360,512]{2,1,0:T(8,128)S(1)}, f32[1,360,512]{2,1,0:T(8,128)}, u32[]{:S(2)}) copy-start(f32[1,360,512]{2,1,0:T(8,128)} %param.9) | copy-start | bytes 2211844
  295.5 54.3 %all-to-all-start.3 = ((bf16[4,12,1,360,128]{4,3,1,2,0:T(8,128)(2,1)}), bf16[4,12,1,360,128]{4,3,1,2,0:T(8,128)(2,1)}, u32[]{:S(2)}, u32[]{:S(2)}) async-start(bf16[4,12,1,360,128]{4,3,1,2,0:T(8,128)(2,1)} %pad_maximum_fusion.1), calls=%async_computation.3 | async-start | bytes 8847360 | tf_op jit(solution)/shard_map/all_to_all | solution.py:93
  300.4 117.4 %all-reduce.2.cloned.1.call-start = ((), (), s32[]{:S(2)}) async-start(), calls=%async_computation.5 | async-start | bytes 1474560 | tf_op jit(solution)/shard_map/psum | solution.py:97
  349.8 4.8 %copy-start = (f32[12,4,360,128]{3,2,1,0:T(8,128)S(1)}, f32[12,4,360,128]{3,2,1,0:T(8,128)}, u32[]{:S(2)}) copy-start(f32[12,4,360,128]{3,2,1,0:T(8,128)} %copy.31) | copy-start | bytes 26542084
Sparse Core Ops, SparseCore 0:
  398.8 19.0 all-reduce.1
